TPU v7x, 32 devices: a whole 2x2x4 slice. The times are simulated.
32 devices in a mesh: freq: 8 (over z, x), sens: 4 (over y, core).
Axes of the slice: x: 2, y: 2, z: 4, core: 2. Of those that a mesh axis runs over, the one named last changes fastest.
Arguments:
- samples: bfloat16 [128, 608, 420], P('freq', 'sens'), may hold values from -6 to 6
- response_tiles: bfloat16 [448, 2, 608, 21], P('freq', None, 'sens'), may hold values from -0.25 to 0.25
- slot_sensor: int32 [608], P('sens'), may hold values from -1 to 599, as said below
- sensor_noise: float32 [600], replicated, may hold values from 0.02 to 5
- advance_offset: int32 [21], replicated, may hold values from 0 to 419
Outputs:
- outlook_values: bfloat16 [128, 21, 420], P('freq')
- noise_spread: float32 [21], replicated
Inputs may be any that keep to these rules, and one draw needn't show every extreme that they name: `slot_sensor`: every sensor number appears in exactly one slot; the other 8 slots hold -1.
All inputs are finite; a program needn't handle non-finite values.
Results may differ from a plain program's by a relative error of at most 0.0055.
Values may be sent and summed in bfloat16 or wider, within the bound.
A program may use at most 64 MiB of HBM per device.

v0:
```python
import math
import jax
import jax.numpy as jnp
from jax import lax
from jax.sharding import PartitionSpec as P

KEPT_HARMONICS = 448


def angles(first_bin, bin_count, period, factor):
    bin_index = first_bin + lax.iota(jnp.int32, bin_count)
    turn_count = bin_index[:, None] * factor[None, :] % period
    return turn_count.astype(jnp.float32) * (2.0 * math.pi / period)


def forward_table(bin_count, step_count, period):
    phase_angle = angles(0, bin_count, period, lax.iota(jnp.int32, step_count))
    return jnp.stack([jnp.cos(phase_angle), -jnp.sin(phase_angle)]).astype(jnp.bfloat16)


def inverse_table(bin_count, step_count, period):
    bin_index = lax.iota(jnp.int32, bin_count)
    weight = jnp.where(bin_index == 0, 1.0, 2.0).astype(jnp.float32) / period
    phase_angle = angles(0, bin_count, period, lax.iota(jnp.int32, step_count))
    return jnp.stack(
        [weight[:, None] * jnp.cos(phase_angle), -weight[:, None] * jnp.sin(phase_angle)]
    )


def contract(spectra, blocks):

    def product(left, right):
        return jnp.einsum("krs,ksq->kqr", left, right, preferred_element_type=jnp.float32)

    real_part = product(spectra[0], blocks[:, 0]) - product(spectra[1], blocks[:, 1])
    imag_part = product(spectra[0], blocks[:, 1]) + product(spectra[1], blocks[:, 0])
    return jnp.stack([real_part, imag_part])


def rotate(summed, first_bin, advance_offset, period):
    twiddle = angles(first_bin, summed.shape[1], period, advance_offset)[:, :, None]
    cosine = jnp.cos(twiddle)
    sine_part = jnp.sin(twiddle)
    real_part = summed[0] * cosine - summed[1] * sine_part
    imag_part = summed[0] * sine_part + summed[1] * cosine
    return jnp.stack([real_part, imag_part])


def on_device(samples, response_tiles, slot_sensor, sensor_noise, advance_offset):
    highest = lax.Precision.HIGHEST
    bins_dev = response_tiles.shape[0]
    first_bin = lax.axis_index("freq") * bins_dev
    period = 2 * KEPT_HARMONICS
    step_count = samples.shape[2]
    live_slot = (slot_sensor >= 0).astype(jnp.bfloat16)
    blocks = response_tiles * live_slot[None, None, :, None]
    sensor_ids = lax.iota(jnp.int32, sensor_noise.shape[0])
    slot_noise = jnp.sum(
        jnp.where(
            slot_sensor[:, None] == sensor_ids[None, :], sensor_noise[None, :], jnp.float32(0.0)
        ),
        axis=1,
    )
    wide = blocks.astype(jnp.float32)
    power = wide[:, 0] * wide[:, 0] + wide[:, 1] * wide[:, 1]
    bin_index = first_bin + lax.iota(jnp.int32, bins_dev)
    bin_weight = jnp.where(bin_index == 0, 1.0, 2.0).astype(jnp.float32) / period
    per_bin = jnp.einsum("ksq,s->kq", power, slot_noise, precision=highest)
    noise_spread = lax.psum(jnp.dot(bin_weight, per_bin, precision=highest), ("freq", "sens"))
    forward = forward_table(KEPT_HARMONICS, step_count, period)
    spectra = jnp.einsum(
        "rst,ckt->ckrs", samples, forward, preferred_element_type=jnp.float32
    ).astype(jnp.bfloat16)
    partial_value = contract(spectra, lax.all_gather(blocks, "freq", axis=0, tiled=True))
    base_bin = 0
    backward = inverse_table(KEPT_HARMONICS, step_count, period)
    summed = lax.psum(partial_value, "sens")
    shifted = rotate(summed, base_bin, advance_offset, period)
    kept_entries_local = jnp.einsum("ckqr,ckt->rqt", shifted, backward, precision=highest)
    outlook_values = kept_entries_local.astype(jnp.bfloat16)
    return (outlook_values, noise_spread)


def solution(mesh):
    placed = (P("freq", "sens", None), P("freq", None, "sens", None), P("sens"), P(), P())
    return jax.shard_map(
        on_device,
        mesh=mesh,
        in_specs=placed,
        out_specs=(P("freq", None, None), P()),
        check_vma=False,
    )
```

profile of v0, /device:TPU:0, one launch (start us, length us, event | category | flops | bytes accessed | tf_op | source)
XLA Modules:
  0.0 256.4 jit_solution(4376142394990606409)
XLA Ops:
  7.2 0.0 all-gather.2.cloned.1.call-start
  7.2 0.8 compare_convert_fusion
  8.1 3.6 %fusion.59 = (f32[56,2,152,21]{2,3,0,1:T(8,128)}, bf16[56,2,152,21]{2,3,0,1:T(8,128)(2,1)}) fusion(bf16[152]{0:T(256)(128)(2,1)S(1)} %compare_convert_fusion, bf16[56,2,152,21]{2,1,3,0:T(2,128)(2,1)} %param.6), kind=kLoop, calls=%fused_computation.80 | loop fusion | flops 715008 | bytes 2860336 | tf_op jit(solution)/shard_map/convert_element_type | solution.py:64
  11.7 0.0 all-gather.2.cloned.1.call-update
  11.7 0.0 all-reduce.2.cloned.1.call-start
  11.8 0.2 select_reduce_fusion
  12.0 1.9 fusion.10
  13.9 1.9 fusion.17
  15.8 0.1 copy.35
  15.9 0.1 convolution_bitcast_fusion
  16.1 45.9 %psum.15 = f32[21]{0:T(128)} all-reduce(f32[21]{0:T(128)S(1)} %convolution_bitcast_fusion), channel_id=1, replica_groups=mesh['freq'=8,'sens'=4] {'freq','sens'}, use_global_device_ids=true, to_apply=%region_2.3 | all-reduce | flops 21 | bytes 168 | tf_op jit(solution)/shard_map/psum | solution.py:69
  62.0 3.8 %negate_convert_fusion = (bf16[1,448,420]{1,2,0:T(8,128)(2,1)S(1)}, bf16[1,448,420]{1,2,0:T(8,128)(2,1)S(1)}) fusion(), kind=kLoop, calls=%fused_computation.36 | loop fusion | flops 2257920 | bytes 752640 | tf_op jit(solution)/shard_map/convert.1
  65.8 2.9 %convolution_convert_fusion = bf16[2,448,16,152]{1,3,2,0:T(8,128)(2,1)S(1)} fusion(bf16[16,152,420]{2,1,0:T(8,128)(2,1)S(1)} %copy-done, bf16[1,448,420]{1,2,0:T(8,128)(2,1)S(1)} %get-tuple-element.16, bf16[1,448,420]{1,2,0:T(8,128)(2,1)S(1)} %get-tuple-element.17), kind=kOutput, calls=%fused_computation.8 | convolution fusion | flops 1834104832 | bytes 7153664 | tf_op jit(solution)/shard_map/rst,ckt->ckrs/dot_general | solution.py:71
  68.7 2.6 %slice_bitcast_fusion.7 = (bf16[448,16,152]{0,2,1:T(8,128)(2,1)}, bf16[448,16,152]{0,2,1:T(8,128)(2,1)}) fusion(bf16[2,448,16,152]{1,3,2,0:T(8,128)(2,1)S(1)} %convolution_convert_fusion), kind=kLoop, calls=%fused_computation.10 | loop fusion | bytes 8716288 | tf_op jit(solution)/shard_map/squeeze | solution.py:35
  71.3 7.4 %copy.24 = bf16[448,16,152]{2,1,0:T(8,128)(2,1)} copy(bf16[448,16,152]{0,2,1:T(8,128)(2,1)} %get-tuple-element.8) | data formatting | bytes 4358144 | tf_op jit(solution)/shard_map/squeeze | solution.py:35
  78.8 7.5 %copy.25 = bf16[448,16,152]{2,1,0:T(8,128)(2,1)} copy(bf16[448,16,152]{0,2,1:T(8,128)(2,1)} %get-tuple-element.9) | data formatting | bytes 4358144 | tf_op jit(solution)/shard_map/squeeze | solution.py:35
  86.3 86.1 %all-gather.2.cloned.1.call-done = bf16[448,2,152,21]{2,3,0,1:T(8,128)(2,1)} async-done(((bf16[56,2,152,21]{2,3,0,1:T(8,128)(2,1)}), bf16[448,2,152,21]{2,3,0,1:T(8,128)(2,1)}) %all-gather.2.cloned.1.call-update) | async-done | bytes 5720080 | tf_op jit(solution)/shard_map/all_gather | solution.py:74
  172.4 5.3 %fusion = f32[448,21,16]{1,2,0:T(8,128)S(1)} fusion(bf16[448,16,152]{2,1,0:T(8,128)(2,1)} %copy.25, bf16[448,2,152,21]{2,3,0,1:T(8,128)(2,1)} %all-gather.2.cloned.1.call-done), kind=kOutput, calls=%fused_computation.2 | convolution fusion | flops 45760512 | bytes 9777152 | tf_op jit(solution)/shard_map/krs,ksq->kqr/dot_general | solution.py:33
  177.8 1.4 copy-done.1
  179.2 5.5 %add_bitcast_fusion = f32[1,448,21,16]{2,3,1,0:T(8,128)} fusion(f32[448,21,16]{1,2,0:T(8,128)S(1)} %fusion, bf16[448,16,152]{2,1,0:T(8,128)(2,1)} %copy.24, bf16[448,2,152,21]{2,3,0,1:T(8,128)(2,1)S(1)} %copy-done.1), kind=kOutput, calls=%fused_computation.6 | convolution fusion | flops 45911040 | bytes 11956224 | tf_op jit(solution)/shard_map/krs,ksq->kqr/dot_general | solution.py:33
  184.7 3.0 %copy.29 = f32[1,448,21,16]{1,3,2,0:T(8,128)S(1)} copy(f32[1,448,21,16]{2,3,1,0:T(8,128)} %add_bitcast_fusion) | data formatting | bytes 1204224 | tf_op jit(solution)/shard_map/stack | solution.py:37
  187.7 5.3 %fusion.1 = f32[448,21,16]{1,2,0:T(8,128)S(1)} fusion(bf16[448,16,152]{2,1,0:T(8,128)(2,1)} %copy.24, bf16[448,2,152,21]{2,3,0,1:T(8,128)(2,1)} %all-gather.2.cloned.1.call-done), kind=kOutput, calls=%fused_computation.3 | convolution fusion | flops 45760512 | bytes 9777152 | tf_op jit(solution)/shard_map/krs,ksq->kqr/dot_general | solution.py:33
  193.0 6.1 %subtract_bitcast_fusion = f32[1,448,21,16]{2,3,1,0:T(8,128)} fusion(f32[448,21,16]{1,2,0:T(8,128)S(1)} %fusion.1, bf16[448,16,152]{2,1,0:T(8,128)(2,1)S(1)} %copy-done.2, bf16[448,2,152,21]{2,3,0,1:T(8,128)(2,1)} %all-gather.2.cloned.1.call-done), kind=kOutput, calls=%fused_computation.7 | convolution fusion | flops 45911040 | bytes 8888320 | tf_op jit(solution)/shard_map/krs,ksq->kqr/dot_general | solution.py:33
  199.2 3.7 %copy.28 = f32[1,448,21,16]{1,3,2,0:T(8,128)} copy(f32[1,448,21,16]{2,3,1,0:T(8,128)} %subtract_bitcast_fusion) | data formatting | bytes 1204224 | tf_op jit(solution)/shard_map/stack | solution.py:37
  202.8 2.4 pad_maximum_fusion
  205.2 0.3 fusion.39
  205.5 4.5 %fusion.31 = (f32[1,448,420]{1,2,0:T(8,128)S(1)}, f32[1,448,420]{1,2,0:T(8,128)}) fusion(f32[448]{0:T(512)S(1)} %select_multiply_fusion, f32[448]{0:T(512)S(1)} %fusion.42), kind=kLoop, calls=%fused_computation.43 | loop fusion | flops 2069760 | bytes 1508864 | tf_op jit(solution)/shard_map/mul | solution.py:26
  210.0 33.6 %all-reduce.2.cloned.1.call-done = f32[2,448,21,16]{1,3,2,0:T(8,128)} async-done(((f32[2,448,21,16]{1,3,2,0:T(8,128)}), f32[2,448,21,16]{1,3,2,0:T(8,128)}) %all-reduce.2.cloned.1.call-update) | async-done | bytes 1204240 | tf_op jit(solution)/shard_map/psum | solution.py:77
  243.6 1.6 multiply_subtract_fusion
  245.2 0.1 pad_maximum_fusion.1
  245.3 3.4 %fusion.19 = bf16[16,21,420]{2,1,0:T(8,128)(2,1)S(1)} fusion(f32[2,448,21,16]{1,3,2,0:T(8,128)S(1)} %pad_maximum_fusion.1, f32[1,448,420]{1,2,0:T(8,128)S(1)} %copy-done.3, f32[1,448,420]{1,2,0:T(8,128)S(1)} %get-tuple-element.18), kind=kOutput, calls=%fused_computation.29 | convolution fusion | flops 1517839616 | bytes 2991744 | tf_op jit(solution)/shard_map/ckqr,ckt->rqt/dot_general | solution.py:79
  248.7 0.8 copy.31
  (16 shorter events, 0.1 us)
Async XLA Ops:
  7.2 58.6 %copy-start = (bf16[16,152,420]{2,1,0:T(8,128)(2,1)S(1)}, bf16[16,152,420]{2,1,0:T(8,128)(2,1)}, u32[]{:S(2)}) copy-start(bf16[16,152,420]{2,1,0:T(8,128)(2,1)} %param.5) | copy-start | bytes 6128644
  7.2 165.2 %all-gather.2.cloned.1.call-start = ((), (), s32[]{:S(2)}) async-start(), calls=%async_computation | async-start | bytes 12386304 | tf_op jit(solution)/shard_map/all_gather | solution.py:74
  8.1 3.7 %copy-start.4 = (f32[600]{0:T(1024)S(1)}, f32[600]{0:T(1024)}, u32[]{:S(2)}) copy-start(f32[600]{0:T(1024)} %param.8) | copy-start | bytes 7204
  8.1 3.7 %copy-start.5 = (s32[152]{0:T(256)S(1)}, s32[152]{0:T(256)}, u32[]{:S(2)}) copy-start(s32[152]{0:T(256)} %param.7) | copy-start | bytes 1828
  11.7 231.8 %all-reduce.2.cloned.1.call-start = ((), (), s32[]{:S(2)}) async-start(), calls=%async_computation.1 | async-start | bytes 2752512 | tf_op jit(solution)/shard_map/psum | solution.py:77
  172.4 6.8 %copy-start.1 = (bf16[448,2,152,21]{2,3,0,1:T(8,128)(2,1)S(1)}, bf16[448,2,152,21]{2,3,0,1:T(8,128)(2,1)}, u32[]{:S(2)}) copy-start(bf16[448,2,152,21]{2,3,0,1:T(8,128)(2,1)} %all-gather.2.cloned.1.call-done) | copy-start | bytes 17160196
  187.7 5.4 %copy-start.2 = (bf16[448,16,152]{2,1,0:T(8,128)(2,1)S(1)}, bf16[448,16,152]{2,1,0:T(8,128)(2,1)}, u32[]{:S(2)}) copy-start(bf16[448,16,152]{2,1,0:T(8,128)(2,1)} %copy.25) | copy-start | bytes 6537220
  202.8 2.4 copy-start.6
  243.6 1.7 copy-start.3
Sparse Core Ops, SparseCore 0:
  11.9 160.5 all-gather.1
  205.3 38.1 all-reduce.1
where the time goes:
time: 257 us; the launch traced here: 256 us
  waiting for transfers between devices  120 us (47%)
  blocking collectives  45.9 us (18%)
  matrix products  30.6 us (12%)
  local copies, waits for them, and re-layouts  26.6 us (10%)
  other arithmetic  19.2 us (7%)
  between operations  14.2 us (6%)
    all_gather x1, waiting for transfers between devices, on_device(): lax.all_gather(blocks, 'freq', axis=0, tiled=True)  86.1 us
    psum x1, blocking collectives, on_device(): lax.psum(jnp.dot(bin_weight, per_bin, precision=highest), ('freq', 'sens'))  45.9 us
    psum x1, waiting for transfers between devices, on_device(): summed = lax.psum(partial_value, 'sens')  33.6 us
    dot_general x4, matrix products, product(): jnp.einsum('krs,ksq->kqr', left, right, preferred_element_type=jnp.float32)  22.3 us
    squeeze x2, local copies, waits for them, and re-layouts, contract(): spectra[0]  10 us
    squeeze x1, local copies, waits for them, and re-layouts, contract(): spectra[1]  7.52 us
    another operation x2, local copies, waits for them, and re-layouts, contract(): return jnp.stack([real_part, imag_part])  6.64 us
  transfers between devices with their start and end apart: 2, of which 2 were waited for; matrix products, arithmetic and copies ran while one was open for 13% of the time, Pallas kernels for 0%

commit v1 on v0

--- a/solution.py
+++ b/solution.py
@@ -71,7 +71,12 @@
     spectra = jnp.einsum(
         "rst,ckt->ckrs", samples, forward, preferred_element_type=jnp.float32
     ).astype(jnp.bfloat16)
-    partial_value = contract(spectra, lax.all_gather(blocks, "freq", axis=0, tiled=True))
+    partial_value = contract(
+        spectra,
+        jnp.concatenate(
+            lax.all_to_all(jnp.stack([blocks] * lax.axis_size("freq")), "freq", 0, 0), axis=0
+        ),
+    )
     base_bin = 0
     backward = inverse_table(KEPT_HARMONICS, step_count, period)
     summed = lax.psum(partial_value, "sens")

time: 257 us -> 363 us (1.41)
  blocking collectives: 45.9 us -> 226 us
  waiting for transfers between devices: 120 us -> 35.2 us
  local copies, waits for them, and re-layouts: 26.6 us -> 35.9 us
  starting transfers between devices: 0.08 us -> 7.45 us
    psum x1, blocking collectives: 45.9 us -> 226 us  [on_device(): lax.psum(jnp.dot(bin_weight, per_bin, precision=highest), ('freq', 'sens'))]
    all_gather x1 -> x0, waiting for transfers between devices: 86.1 us -> none  [on_device(): lax.all_gather(blocks, 'freq', axis=0, tiled=True)]
    all_to_all x0 -> x1, starting transfers between devices: none -> 7.41 us  [on_device(): lax.all_to_all(jnp.stack([blocks] * lax.axis_size('freq')), 'freq', 0, 0)]
    all_to_all x0 -> x1, local copies, waits for them, and re-layouts: none -> 7.12 us  [on_device(): lax.all_to_all(jnp.stack([blocks] * lax.axis_size('freq')), 'freq', 0, 0)]
    another operation x0 -> x1, local copies, waits for them, and re-layouts: none -> 4.3 us  [on_device(): jnp.stack([blocks] * lax.axis_size('freq'))]
    dot_general x4, matrix products: 22.3 us -> 18.4 us  [product(): jnp.einsum('krs,ksq->kqr', left, right, preferred_element_type=jnp.float32)]
  transfers between devices with their start and end apart: 2 -> 2, of which waited for: 2 -> 1; matrix products, arithmetic and copies ran while one was open for 13% -> 8% of each run, Pallas kernels for 0% -> 0%
where the time goes in v1:
time: 363 us
  blocking collectives  226 us (62%)
  local copies, waits for them, and re-layouts  35.9 us (10%)
  waiting for transfers between devices  35.2 us (10%)
  matrix products  28.2 us (8%)
  other arithmetic  15.7 us (4%)
  between operations  14.2 us (4%)
  starting transfers between devices  7.45 us (2%)
    psum x1, blocking collectives, on_device(): lax.psum(jnp.dot(bin_weight, per_bin, precision=highest), ('freq', 'sens'))  226 us
    psum x1, waiting for transfers between devices, on_device(): summed = lax.psum(partial_value, 'sens')  35.2 us
    dot_general x4, matrix products, product(): jnp.einsum('krs,ksq->kqr', left, right, preferred_element_type=jnp.float32)  18.4 us
    squeeze x2, local copies, waits for them, and re-layouts, contract(): spectra[0]  9.33 us
    all_to_all x1, starting transfers between devices, on_device(): lax.all_to_all(jnp.stack([blocks] * lax.axis_size('freq')), 'freq', 0, 0)  7.41 us
  transfers between devices with their start and end apart: 2, of which 1 were waited for; matrix products, arithmetic and copies ran while one was open for 8% of the time, Pallas kernels for 0%

profile of v1, /device:TPU:0, one launch (start us, length us, event | category | flops | bytes accessed | tf_op | source)
XLA Modules:
  0.0 362.8 jit_solution(15439174408532347498)
XLA Ops:
  7.2 0.8 compare_convert_fusion
  8.0 3.0 fusion.59
  11.0 4.3 %stack.16 = bf16[8,56,2,152,21]{3,1,4,2,0:T(8,128)(2,1)} broadcast(bf16[56,2,152,21]{2,0,3,1:T(8,128)(2,1)S(1)} %get-tuple-element.11), dimensions={1,2,3,4} | broadcast | bytes 6435072 | tf_op jit(solution)/shard_map/stack | solution.py:77
  15.3 7.4 %all-to-all-start = ((bf16[8,56,2,152,21]{3,1,4,2,0:T(8,128)(2,1)}), bf16[8,56,2,152,21]{3,1,4,2,0:T(8,128)(2,1)}, u32[]{:S(2)}, u32[]{:S(2)}) async-start(bf16[8,56,2,152,21]{3,1,4,2,0:T(8,128)(2,1)} %stack.16), calls=%async_computation | async-start | bytes 19267584 | tf_op jit(solution)/shard_map/all_to_all | solution.py:77
  22.8 0.2 select_reduce_fusion
  23.0 3.4 fusion.17
  26.3 0.1 copy.44
  26.4 0.1 convolution_bitcast_fusion
  26.6 226.2 %psum.15 = f32[21]{0:T(128)} all-reduce(f32[21]{0:T(128)S(1)} %convolution_bitcast_fusion), channel_id=1, replica_groups=mesh['freq'=8,'sens'=4] {'freq','sens'}, use_global_device_ids=true, to_apply=%region_2.3 | all-reduce | flops 21 | bytes 168 | tf_op jit(solution)/shard_map/psum | solution.py:69
  252.7 3.8 %negate_convert_fusion = (bf16[1,448,420]{1,2,0:T(8,128)(2,1)S(1)}, bf16[1,448,420]{1,2,0:T(8,128)(2,1)S(1)}) fusion(), kind=kLoop, calls=%fused_computation.35 | loop fusion | flops 2257920 | bytes 752640 | tf_op jit(solution)/shard_map/convert.1
  256.5 2.9 convolution_convert_fusion
  259.5 1.9 slice_bitcast_fusion.7
  261.3 7.4 %copy.34 = bf16[448,16,152]{2,1,0:T(8,128)(2,1)} copy(bf16[448,16,152]{0,2,1:T(8,128)(2,1)} %get-tuple-element.12) | data formatting | bytes 4358144 | tf_op jit(solution)/shard_map/squeeze | solution.py:35
  268.8 5.5 %copy.35 = bf16[448,16,152]{2,1,0:T(8,128)(2,1)} copy(bf16[448,16,152]{0,2,1:T(8,128)(2,1)S(1)} %get-tuple-element.13) | data formatting | bytes 4358144 | tf_op jit(solution)/shard_map/squeeze | solution.py:35
  274.3 7.1 %copy.33 = bf16[8,56,2,152,21]{3,4,1,0,2:T(8,128)(2,1)S(1)} copy(bf16[8,56,2,152,21]{3,1,4,2,0:T(8,128)(2,1)} %all-to-all-done) | data formatting | bytes 11440128 | tf_op jit(solution)/shard_map/all_to_all | solution.py:77
  281.5 3.4 fusion.1
  284.8 1.3 copy-done.4
  286.2 3.4 fusion
  289.6 0.5 copy-done.2
  290.1 0.9 copy-done.5
  291.0 3.4 subtract_bitcast_fusion
  294.3 3.0 copy.38
  297.3 8.2 %add_bitcast_fusion = f32[1,448,21,16]{2,3,1,0:T(8,128)} fusion(f32[448,21,16]{1,2,0:T(8,128)} %fusion, bf16[448,16,152]{2,1,0:T(8,128)(2,1)} %copy.34, bf16[448,2,152,21]{2,3,0,1:T(8,128)(2,1)} %bitcast.67), kind=kOutput, calls=%fused_computation.6 | convolution fusion | flops 45911040 | bytes 13447168 | tf_op jit(solution)/shard_map/krs,ksq->kqr/dot_general | solution.py:33
  305.5 3.0 copy.39
  308.5 1.3 pad_maximum_fusion
  309.8 0.3 fusion.39
  310.1 4.7 %fusion.31 = (f32[1,448,420]{1,2,0:T(8,128)S(1)}, f32[1,448,420]{1,2,0:T(8,128)}) fusion(f32[448]{0:T(512)S(1)} %select_multiply_fusion, f32[448]{0:T(512)S(1)} %fusion.42), kind=kLoop, calls=%fused_computation.42 | loop fusion | flops 2069760 | bytes 1508864 | tf_op jit(solution)/shard_map/mul | solution.py:26
  314.8 35.2 %all-reduce.2.cloned.1.call-done = f32[2,448,21,16]{1,3,2,0:T(8,128)} async-done(((f32[2,448,21,16]{1,3,2,0:T(8,128)}), f32[2,448,21,16]{1,3,2,0:T(8,128)}) %all-reduce.2.cloned.1.call-update) | async-done | bytes 1204240 | tf_op jit(solution)/shard_map/psum | solution.py:82
  350.0 1.6 multiply_subtract_fusion
  351.6 0.1 pad_maximum_fusion.1
  351.7 3.4 fusion.19
  355.1 0.8 copy.41
  (22 shorter events, 0.1 us)
Async XLA Ops:
  7.2 249.3 %copy-start = (bf16[16,152,420]{2,1,0:T(8,128)(2,1)S(1)}, bf16[16,152,420]{2,1,0:T(8,128)(2,1)}, u32[]{:S(2)}) copy-start(bf16[16,152,420]{2,1,0:T(8,128)(2,1)} %param.5) | copy-start | bytes 6128644
  15.3 7.5 %copy-start.7 = (f32[600]{0:T(1024)S(1)}, f32[600]{0:T(1024)}, u32[]{:S(2)}) copy-start(f32[600]{0:T(1024)} %param.8) | copy-start | bytes 7204
  15.3 7.5 %copy-start.8 = (s32[152]{0:T(256)S(1)}, s32[152]{0:T(256)}, u32[]{:S(2)}) copy-start(s32[152]{0:T(256)} %param.7) | copy-start | bytes 1828
  15.3 259.0 %all-to-all-start = ((bf16[8,56,2,152,21]{3,1,4,2,0:T(8,128)(2,1)}), bf16[8,56,2,152,21]{3,1,4,2,0:T(8,128)(2,1)}, u32[]{:S(2)}, u32[]{:S(2)}) async-start(bf16[8,56,2,152,21]{3,1,4,2,0:T(8,128)(2,1)} %stack.16), calls=%async_computation | async-start | bytes 19267584 | tf_op jit(solution)/shard_map/all_to_all | solution.py:77
  22.7 327.3 %all-reduce.2.cloned.1.call-start = ((), (), s32[]{:S(2)}) async-start(), calls=%async_computation.1 | async-start | bytes 2752512 | tf_op jit(solution)/shard_map/psum | solution.py:82
  274.3 7.1 %copy-start.3 = (bf16[448,16,152]{2,1,0:T(8,128)(2,1)S(1)}, bf16[448,16,152]{2,1,0:T(8,128)(2,1)}, u32[]{:S(2)}) copy-start(bf16[448,16,152]{2,1,0:T(8,128)(2,1)} %copy.34) | copy-start | bytes 6537220
  281.4 8.7 %copy-start.2 = (bf16[8,56,2,152,21]{3,4,1,0,2:T(8,128)(2,1)}, bf16[8,56,2,152,21]{3,4,1,0,2:T(8,128)(2,1)S(1)}, u32[]{:S(2)}) copy-start(bf16[8,56,2,152,21]{3,4,1,0,2:T(8,128)(2,1)S(1)} %copy.33) | copy-start | bytes 17160196
  281.4 4.7 %copy-start.4 = (bf16[448,16,152]{2,1,0:T(8,128)(2,1)S(1)}, bf16[448,16,152]{2,1,0:T(8,128)(2,1)}, u32[]{:S(2)}) copy-start(bf16[448,16,152]{2,1,0:T(8,128)(2,1)} %copy.35) | copy-start | bytes 6537220
  286.2 4.8 %copy-start.5 = (f32[448,21,16]{1,2,0:T(8,128)S(1)}, f32[448,21,16]{1,2,0:T(8,128)}, u32[]{:S(2)}) copy-start(f32[448,21,16]{1,2,0:T(8,128)} %fusion.1) | copy-start | bytes 1806340
  305.5 4.3 %copy-start.9 = (s32[21]{0:T(128)S(1)}, s32[21]{0:T(128)}, u32[]{:S(2)}) copy-start(s32[21]{0:T(128)} %param.9) | copy-start | bytes 256
  350.0 1.7 copy-start.6
  351.5 4.4 %copy-start.1 = (bf16[16,152,420]{2,1,0:T(8,128)(2,1)S(1)}, bf16[16,152,420]{2,1,0:T(8,128)(2,1)}, u32[]{:S(2)}) copy-start(bf16[16,152,420]{2,1,0:T(8,128)(2,1)} %param.5) | copy-start | bytes 6128644
Sparse Core Ops, SparseCore 0:
  309.9 39.9 all-reduce.1
